TPU v7x, 32 devices: a whole 2x2x4 slice. The times are simulated.
32 devices in a mesh: freq: 4 (over z), strip: 8 (over y, x, core).
Axes of the slice: x: 2, y: 2, z: 4, core: 2. Of those that a mesh axis runs over, the one named last changes fastest.
Arguments:
- receiver_field: float32 [2, 4, 64, 512], P(None, 'freq', 'strip'), may hold values from -17 to 17
- source_field: float32 [2, 4, 64, 512], P(None, 'freq', 'strip'), may hold values from -4 to 4
- velocity_class: int32 [64, 512], P('strip'), may hold values from 0 to 7
- filters: float32 [4, 8, 2, 9], P('freq'), may hold values from -0.8 to 0.8
- point_spread: float32 [16, 2, 15, 15], replicated, may hold values from -0.05 to 1
- spread_index: int32 [8, 4], replicated, may hold values from 0 to 15
Outputs:
- migrated: float32 [64, 2, 512], P('strip', None, 'freq')
- reflectivity: float32 [64, 2, 512], P('strip', None, 'freq')
- misfit: float32 [], replicated
All inputs are finite; a program needn't handle non-finite values.
Results may differ from a plain program's by a relative error of at most 0.0003.
Values sent between devices are 32-bit elements; how exact they have to be, the bound alone decides.
A program may use at most 64 MiB of HBM per device.

v0:
```python
import functools
import math

import jax
import jax.numpy as jnp
from jax import lax
from jax.experimental import pallas as pl
from jax.experimental.pallas import tpu as pltpu
from jax.sharding import PartitionSpec as P

STEPS = 2
NCLASS = 8
PASSES = 2
MESH = pl.DeviceIdType.MESH


def kernel(
    groups,
    strips,
    near,
    spread_ref,
    filters_ref,
    receiver_ref,
    source_ref,
    class_ref,
    psf_ref,
    migrated_ref,
    reflect_ref,
    misfit_ref,
    rows_out,
    rows_in,
    class_in,
    fields,
    classes,
    shifted,
    coefs,
    terms,
    terms_in,
    own_table,
    table,
    rim_out,
    rim_in,
    rolled,
    spill,
    strip_spill,
    moved,
    sums_out,
    sums_in,
    send_sem,
    recv_sem,
    class_sem,
    rim_sem,
    sum_sem,
):
    freq = lax.axis_index("freq")
    strip = lax.axis_index("strip")
    total = groups * strips
    me = freq * strips + strip
    rows, cols = class_ref.shape
    share = migrated_ref.shape[2]
    side = psf_ref.shape[2]
    reach = side // 2
    wide = 2 * share
    reaches = [(dj, dk) for dj in range(-near, near + 1) for dk in (-1, 0, 1)]
    reaches.remove((0, 0))
    reaches.append((0, 0))
    place = {pair: at for at, pair in enumerate(reaches)}
    partners = len(reaches) - 1
    span = 2 * near + 1

    barrier = pltpu.get_barrier_semaphore()

    def greet(i, carry):
        other = lax.rem(me + i, total)
        pl.semaphore_signal(
            barrier,
            inc=1,
            device_id=(other // strips, lax.rem(other, strips)),
            device_id_type=MESH,
        )
        return carry

    lax.fori_loop(1, total, greet, 0)

    for field, ref in enumerate((receiver_ref, source_ref)):
        for part in range(2):
            at = 2 * (2 * field + part)
            rows_out[0, at : at + 2, :] = ref[part, 0, 0:2, :]
            rows_out[1, at : at + 2, :] = ref[part, 0, rows - 2 : rows, :]

    pl.semaphore_wait(barrier, total - 1)

    up = lax.rem(strip + strips - 1, strips)
    down = lax.rem(strip + 1, strips)
    copies = []
    for side_at, other in ((0, up), (1, down)):
        copies.append(
            pltpu.make_async_remote_copy(
                src_ref=rows_out.at[side_at],
                dst_ref=rows_in.at[side_at],
                send_sem=send_sem.at[side_at],
                recv_sem=recv_sem.at[side_at],
                device_id=(freq, other),
                device_id_type=MESH,
            )
        )
        copies.append(
            pltpu.make_async_remote_copy(
                src_ref=class_ref,
                dst_ref=class_in.at[side_at],
                send_sem=class_sem.at[side_at],
                recv_sem=class_sem.at[2 + side_at],
                device_id=(freq, other),
                device_id_type=MESH,
            )
        )
    for copy in copies:
        copy.start()

    lane = lax.broadcasted_iota(jnp.int32, (1, wide), 1)
    column = jnp.where(lane < wide - wide // 4, lane, lane - wide)

    def spread_of(row_step, col_step):
        row_at = jnp.clip(strip + row_step, 0, strips - 1)
        col_at = jnp.clip(freq + col_step, 0, groups - 1)
        chosen = spread_ref[row_at, col_at]
        both = psf_ref[chosen]
        return both[0] + both[1], both[0] - both[1]

    def fill(j, carry):
        left = spread_of(j - near, -1)
        middle = spread_of(j - near, 0)
        right = spread_of(j - near, 1)
        for st in range(2):
            for b in range(side):
                source_col = column - (b - reach)
                shape = (side, wide)
                k_left = jnp.broadcast_to(left[st][:, b : b + 1], shape)
                k_middle = jnp.broadcast_to(middle[st][:, b : b + 1], shape)
                k_right = jnp.broadcast_to(right[st][:, b : b + 1], shape)
                table[j * 2 + st, b, 0:side, :] = jnp.where(
                    source_col < 0, k_left, jnp.where(source_col >= share, k_right, k_middle)
                )
        return carry

    lax.fori_loop(0, span, fill, 0)
    own = spread_of(0, 0)
    for st in range(2):
        for b in range(side):
            own_table[st, b, 0:side, :] = jnp.broadcast_to(own[st][:, b : b + 1], (side, share))

    for field, ref in enumerate((receiver_ref, source_ref)):
        for part in range(2):
            fields[2 * field + part, rows : 2 * rows, :] = ref[part, 0]
    classes[rows : 2 * rows, :] = class_ref[...]
    for copy in copies:
        copy.wait()
    first = strip == 0
    last = strip == strips - 1
    for comp in range(4):
        above = rows_in[1, 2 * comp : 2 * comp + 2, :]
        below = rows_in[0, 2 * comp : 2 * comp + 2, :]
        fields[comp, rows - 2 : rows, :] = jnp.where(first, 0.0, above)
        fields[comp, 2 * rows : 2 * rows + 2, :] = jnp.where(last, 0.0, below)
    classes[rows - 1 : rows, :] = class_in[1, rows - 1 : rows, :]
    classes[2 * rows : 2 * rows + 1, :] = class_in[0, 0:1, :]

    levels = classes[rows - 1 : 3 * rows - 1, :]
    for part in range(2):
        for tap in range(9):
            value = jnp.full(levels.shape, filters_ref[0, 0, part, tap], jnp.float32)
            for level in range(1, NCLASS):
                value = jnp.where(levels == level, filters_ref[0, level, part, tap], value)
            coefs[part * 9 + tap] = value

    edge = lax.broadcasted_iota(jnp.int32, (1, cols), 1)

    def shift_all():
        for comp in range(4):
            base = fields[comp]
            shifted[comp, 0] = jnp.where(edge == 0, 0.0, pltpu.roll(base, 1, 1))
            shifted[comp, 1] = base
            shifted[comp, 2] = jnp.where(edge == cols - 1, 0.0, pltpu.roll(base, cols - 1, 1))

    def advance(field, start, count, skip):
        factor = 1.0 if field == 0 else -1.0
        real_part = jnp.zeros((count, cols), jnp.float32)
        imag_part = jnp.zeros((count, cols), jnp.float32)
        for tap in range(9):
            at = start + tap // 3 - 1
            near_real = shifted[2 * field, tap % 3, at : at + count, :]
            near_imag = shifted[2 * field + 1, tap % 3, at : at + count, :]
            coef_real = coefs[tap, skip : skip + count, :]
            coef_imag = factor * coefs[9 + tap, skip : skip + count, :]
            real_part = real_part + coef_real * near_real - coef_imag * near_imag
            imag_part = imag_part + coef_real * near_imag + coef_imag * near_real
        return real_part, imag_part

    shift_all()
    line = lax.broadcasted_iota(jnp.int32, (2 * rows, cols), 0)
    alive = (line < rows + 2) & ((line > 0) | (strip > 0)) & ((line < rows + 1) | (strip < strips - 1))
    ahead = advance(0, rows - 1, 2 * rows, 0) + advance(1, rows - 1, 2 * rows, 0)
    for comp in range(4):
        fields[comp, rows - 1 : 3 * rows - 1, :] = jnp.where(alive, ahead[comp], 0.0)
    shift_all()
    second = advance(0, rows, rows, 1) + advance(1, rows, rows, 1)
    firsts = [fields[comp, rows : 2 * rows, :] for comp in range(4)]
    for depth, f in enumerate((firsts, second)):
        image = f[0] * f[2] + f[1] * f[3]
        for g in range(groups):
            terms[g, depth] = image[:, g * share : (g + 1) * share]

    def send_terms(i, carry):
        other = lax.rem(freq + i, groups)
        pltpu.make_async_remote_copy(
            src_ref=terms.at[other],
            dst_ref=terms_in.at[i - 1],
            send_sem=send_sem.at[2],
            recv_sem=recv_sem.at[2],
            device_id=(other, strip),
            device_id_type=MESH,
        ).start()
        return carry

    def wait_all(buffer, sem):
        pltpu.make_async_copy(buffer, buffer, sem).wait()

    lax.fori_loop(1, groups, send_terms, 0)
    wait_all(terms_in, recv_sem.at[2])
    scaling = 1.0 / math.sqrt(groups)
    migrated = terms[freq]
    for i in range(groups - 1):
        migrated = migrated + terms_in[i]
    migrated = migrated * scaling
    for depth in range(STEPS):
        migrated_ref[:, depth, :] = migrated[depth]

    def send_rim(value, turn):
        rim_out[turn] = value
        rim_in[turn, partners] = value
        for dj, dk in reaches[:-1]:
            pltpu.make_async_remote_copy(
                src_ref=rim_out.at[turn],
                dst_ref=rim_in.at[turn, place[(-dj, -dk)]],
                send_sem=rim_sem.at[2 * turn],
                recv_sem=rim_sem.at[2 * turn + 1],
                device_id=(
                    lax.rem(freq + dk + groups, groups),
                    lax.rem(strip + dj + near * strips, strips),
                ),
                device_id_type=MESH,
            ).start()

    quarter = share // 4
    slim = lax.broadcasted_iota(jnp.int32, (1, share), 1)

    def send_sums(parts, turn):
        row = jnp.zeros((1, share), jnp.float32)
        for at, part in enumerate(parts):
            lanes = jnp.sum(part, axis=0, keepdims=True)
            lanes = lanes + pltpu.roll(lanes, share // 2, 1)
            lanes = lanes + pltpu.roll(lanes, quarter, 1)
            row = jnp.where((slim >= at * quarter) & (slim < (at + 1) * quarter), lanes, row)
        sums_out[turn] = row

        def send(i, carry):
            other = lax.rem(me + i, total)
            pltpu.make_async_remote_copy(
                src_ref=sums_out.at[turn],
                dst_ref=sums_in.at[turn, i - 1],
                send_sem=sum_sem.at[2 * turn],
                recv_sem=sum_sem.at[2 * turn + 1],
                device_id=(other // strips, lax.rem(other, strips)),
                device_id_type=MESH,
            ).start()
            return carry

        lax.fori_loop(1, total, send, 0)
        return row

    def take_sums(row, turn, count):
        wait_all(sums_in.at[turn], sum_sem.at[2 * turn + 1])
        row = row + jnp.sum(sums_in[turn], axis=0)
        return [
            jnp.sum(
                jnp.where((slim >= at * quarter) & (slim < (at + 1) * quarter), row, 0.0),
                axis=1,
                keepdims=True,
            )
            for at in range(count)
        ]

    def rim_values(turn):
        found = []
        for dj in range(-near, near + 1):
            ok = (strip + dj >= 0) & (strip + dj < strips)
            pair = []
            for depth in range(STEPS):
                middle = jnp.where(ok, rim_in[turn, place[(dj, 0)], depth], 0.0)
                right = jnp.where(ok & (freq < groups - 1), rim_in[turn, place[(dj, 1)], depth], 0.0)
                left = jnp.where(ok & (freq > 0), rim_in[turn, place[(dj, -1)], depth], 0.0)
                outer = jnp.where(
                    slim < 2 * reach, right, jnp.where(slim >= share - 2 * reach, left, 0.0)
                )
                pair.append(jnp.concatenate([middle, outer], axis=1))
            found.append(pair)
        return found

    tall = 3 * rows

    def descend(weighted):
        for j in range(span):
            for st in range(2):
                both = weighted[j][0] + weighted[j][1] if st == 0 else weighted[j][0] - weighted[j][1]
                for b in range(side):
                    rolled[2 * j + st, b] = pltpu.roll(both, (b - reach) % wide, 1)
        spill[...] = jnp.zeros_like(spill)

        def one(index, carry):
            j = index // 2
            st = lax.rem(index, 2)
            strip_spill[...] = jnp.zeros_like(strip_spill)
            for low in (0, 5, 10):
                high = min(low + 5, side)
                totals = [jnp.zeros((rows, wide), jnp.float32) for a in range(low, high)]
                for b in range(side):
                    data = rolled[index, b]
                    for a in range(low, high):
                        totals[a - low] = totals[a - low] + table[index, b, a : a + 1, :] * data
                for a in range(low, high):
                    strip_spill[a : a + rows, :] += totals[a - low]
            at = pl.ds(pl.multiple_of(rows * j, rows), tall)
            spill[st, at, :] += strip_spill[...]
            return carry

        lax.fori_loop(0, 2 * span, one, 0)
        depth_line = lax.broadcasted_iota(jnp.int32, (tall, wide), 0) - reach + strip * rows
        at_col = column + freq * share
        ok = (
            (depth_line >= 0)
            & (depth_line < strips * rows)
            & (at_col >= 0)
            & (at_col < groups * share)
        )
        base = near * rows
        values = [jnp.where(ok, spill[st, base : base + tall, :], 0.0) for st in range(2)]
        for st in range(2):
            spill[st, base : base + tall, :] = values[st]
        mine = [spill[st, base + reach : base + reach + rows, 0:share] for st in range(2)]
        descent = [0.5 * (mine[0] + mine[1]), 0.5 * (mine[0] - mine[1])]
        image = [jnp.zeros((rows, share), jnp.float32) for st in range(2)]
        for st in range(2):
            for b in range(side):
                moved[st, b] = pltpu.roll(values[st], (reach - b) % wide, 1)[:, 0:share]
            for b in range(side):
                for a in range(side):
                    image[st] = image[st] + own_table[st, b, a : a + 1, :] * moved[st, b, a : a + rows, :]
        image_of = [0.5 * (image[0] + image[1]), 0.5 * (image[0] - image[1])]
        return descent, image_of

    cells = float(STEPS * rows * strips * cols)
    send_rim(-migrated, 0)
    row = send_sums([migrated[0] * migrated[0] + migrated[1] * migrated[1]], 0)
    wait_all(rim_in.at[0, 0:partners], rim_sem.at[1])
    residual = rim_values(0)
    (energy,) = take_sums(row, 0, 1)
    reflect = [jnp.zeros((rows, share), jnp.float32) for depth in range(STEPS)]
    for turn in range(1, PASSES + 1):
        weights = [
            [1.0 / jnp.sqrt(r * r + energy / cells) for r in pair] for pair in residual
        ]
        weighted = [[w * r for w, r in zip(ws, rs)] for ws, rs in zip(weights, residual)]
        descent, image_of = descend(weighted)
        if turn < PASSES:
            send_rim(jnp.stack(image_of), turn)
        parts = [jnp.zeros((rows, share), jnp.float32) for q in range(4)]
        for depth in range(STEPS):
            v = image_of[depth]
            r = residual[near][depth][:, 0:share]
            w = weights[near][depth][:, 0:share]
            parts[0] = parts[0] + descent[depth] * descent[depth]
            parts[1] = parts[1] + w * v * v
            parts[2] = parts[2] + r * v
            parts[3] = parts[3] + v * v
        row = send_sums(parts, turn)
        if turn < PASSES:
            wait_all(rim_in.at[turn, 0:partners], rim_sem.at[2 * turn + 1])
            images = rim_values(turn)
        grad_square, curvature, cross_term, power_term = take_sums(row, turn, 4)
        step_length = grad_square / curvature
        energy = energy - 2.0 * step_length * cross_term + step_length * step_length * power_term
        reflect = [x - step_length * d for x, d in zip(reflect, descent)]
        if turn < PASSES:
            residual = [
                [r - step_length * v for r, v in zip(rs, vs)] for rs, vs in zip(residual, images)
            ]
    for depth in range(STEPS):
        reflect_ref[:, depth, :] = reflect[depth]
    misfit_ref[...] = energy / cells

    wait_all(terms_in, send_sem.at[2])
    for turn in range(PASSES):
        wait_all(rim_in.at[turn, 0:partners], rim_sem.at[2 * turn])
    for turn in range(PASSES + 1):
        wait_all(sums_in.at[turn], sum_sem.at[2 * turn])


def local(receiver_field, source_field, velocity_class, filters, point_spread, spread_index):
    groups = lax.axis_size("freq")
    strips = lax.axis_size("strip")
    rows, cols = velocity_class.shape
    share = cols // groups
    side = point_spread.shape[2]
    reach = side // 2
    near = -(-2 * reach // rows)
    partners = 3 * (2 * near + 1) - 1
    total = groups * strips
    wide = 2 * share
    vmem = pl.BlockSpec(memory_space=pltpu.VMEM)
    smem = pl.BlockSpec(memory_space=pltpu.SMEM)
    f32 = jnp.float32
    dma = pltpu.SemaphoreType.DMA
    deep = -(-(rows * (2 * near + 1) + side) // 8) * 8
    migrated, reflectivity, misfit = pl.pallas_call(
        functools.partial(kernel, groups, strips, near),
        out_shape=(
            jax.ShapeDtypeStruct((rows, STEPS, share), f32),
            jax.ShapeDtypeStruct((rows, STEPS, share), f32),
            jax.ShapeDtypeStruct((1, 1), f32),
        ),
        in_specs=[smem, smem, vmem, vmem, vmem, vmem],
        out_specs=(vmem, vmem, vmem),
        scratch_shapes=[
            pltpu.VMEM((2, 8, cols), f32),
            pltpu.VMEM((2, 8, cols), f32),
            pltpu.VMEM((2, rows, cols), jnp.int32),
            pltpu.VMEM((4, 3 * rows, cols), f32),
            pltpu.VMEM((3 * rows, cols), jnp.int32),
            pltpu.VMEM((4, 3, 3 * rows, cols), f32),
            pltpu.VMEM((18, 2 * rows, cols), f32),
            pltpu.VMEM((groups, STEPS, rows, share), f32),
            pltpu.VMEM((groups - 1, STEPS, rows, share), f32),
            pltpu.VMEM((2, side, 16, share), f32),
            pltpu.VMEM((2 * (2 * near + 1), side, 16, wide), f32),
            pltpu.VMEM((PASSES, STEPS, rows, share), f32),
            pltpu.VMEM((PASSES, partners + 1, STEPS, rows, share), f32),
            pltpu.VMEM((2 * (2 * near + 1), side, rows, wide), f32),
            pltpu.VMEM((2, deep, wide), f32),
            pltpu.VMEM((3 * rows, wide), f32),
            pltpu.VMEM((2, side, 3 * rows, share), f32),
            pltpu.VMEM((PASSES + 1, 1, share), f32),
            pltpu.VMEM((PASSES + 1, total - 1, 1, share), f32),
            dma((3,)),
            dma((3,)),
            dma((4,)),
            dma((2 * PASSES,)),
            dma((2 * (PASSES + 1),)),
        ],
        compiler_params=pltpu.CompilerParams(collective_id=0, has_side_effects=True),
    )(spread_index, filters, receiver_field, source_field, velocity_class, point_spread)
    return migrated, reflectivity, misfit[0, 0]


def solution(mesh):
    return jax.shard_map(
        local,
        mesh=mesh,
        in_specs=(
            P(None, "freq", "strip", None),
            P(None, "freq", "strip", None),
            P("strip", None),
            P("freq", None, None, None),
            P(),
            P(),
        ),
        out_specs=(P("strip", None, "freq"), P("strip", None, "freq"), P()),
        check_vma=False,
    )
```

profile of v0, /device:TPU:0, one launch (start us, length us, event | category | flops | bytes accessed | tf_op | source)
XLA Modules:
  0.0 45.0 jit_solution(14895404701758768309)
XLA Ops:
  0.6 1.3 %copy.9.spread_ref = s32[8,4]{1,0:T(8,128)} copy(s32[8,4]{0,1:T(4,128)} %param.11) | data formatting | bytes 256 | tf_op args[5]
  2.0 1.9 %copy.10.psf_ref = f32[16,2,15,15]{3,2,1,0:T(8,128)} copy(f32[16,2,15,15]{0,1,3,2:T(2,128)} %param.10) | data formatting | bytes 57600 | tf_op args[4]
  3.9 37.3 %shard_map.85 = (f32[8,2,128]{2,1,0:T(2,128)}, f32[8,2,128]{2,1,0:T(2,128)}, f32[1,1]{1,0:T(1,128)}) custom-call(s32[8,4]{1,0:T(8,128)} %copy.9.spread_ref, f32[1,8,2,9]{3,2,1,0:T(2,128)} %filters_ref.1, f32[2,1,8,512]{3,2,1,0:T(8,128)} %receiver_ref.1, f32[2,1,8,512]{3,2,1,0:T(8,128)} %source_ref.1, s32[8,512]{1,0:T(8,128)} %class_ref.1, ...), custom_call_target="tpu_custom_call" | custom-call | tf_op jit(solution)/shard_map/pallas_call | solution.py:424
  41.3 0.0 copy-start
  41.3 1.3 %copy.14 = f32[8,2,128]{2,1,0:T(2,128)} copy(f32[8,2,128]{2,1,0:T(2,128)} %get-tuple-element.12) | data formatting | bytes 16384
  42.6 0.0 copy-done
  42.6 0.6 %copy.15 = f32[8,2,128]{2,1,0:T(2,128)} copy(f32[8,2,128]{2,1,0:T(2,128)S(1)} %copy-done) | data formatting | bytes 16384
Async XLA Ops:
  41.3 1.3 %copy-start = (f32[8,2,128]{2,1,0:T(2,128)S(1)}, f32[8,2,128]{2,1,0:T(2,128)}, u32[]{:S(2)}) copy-start(f32[8,2,128]{2,1,0:T(2,128)} %get-tuple-element.13) | copy-start | bytes 24580
where the time goes:
time: 45.2 us; the launch traced here: 45 us
  Pallas kernels  37.3 us (83%)
  local copies, waits for them, and re-layouts  5.2 us (12%)
  between operations  2.47 us (5%)
    pallas_call x1, Pallas kernels, local(): pl.pallas_call(functools.partial(kernel, groups, strips, near), out_shape...  37.3 us
    unnamed x6, local copies, waits for them, and re-layouts  5.2 us

commit v1 on v0

--- a/solution.py
+++ b/solution.py
@@ -29,6 +29,7 @@
     misfit_ref,
     rows_out,
     rows_in,
+    class_out,
     class_in,
     fields,
     classes,
@@ -36,6 +37,7 @@
     coefs,
     terms,
     terms_in,
+    by_index,
     own_table,
     table,
     rim_out,
@@ -58,7 +60,8 @@
     me = freq * strips + strip
     rows, cols = class_ref.shape
     share = migrated_ref.shape[2]
-    side = psf_ref.shape[2]
+    side = psf_ref.shape[0]
+    count = psf_ref.shape[3]
     reach = side // 2
     wide = 2 * share
     reaches = [(dj, dk) for dj in range(-near, near + 1) for dk in (-1, 0, 1)]
@@ -70,17 +73,20 @@
 
     barrier = pltpu.get_barrier_semaphore()
 
-    def greet(i, carry):
-        other = lax.rem(me + i, total)
+    for i in range(1, groups):
         pl.semaphore_signal(
             barrier,
             inc=1,
-            device_id=(other // strips, lax.rem(other, strips)),
+            device_id=(lax.rem(freq + i, groups), strip),
             device_id_type=MESH,
         )
-        return carry
-
-    lax.fori_loop(1, total, greet, 0)
+    for i in range(1, strips):
+        pl.semaphore_signal(
+            barrier,
+            inc=1,
+            device_id=(freq, lax.rem(strip + i, strips)),
+            device_id_type=MESH,
+        )
 
     for field, ref in enumerate((receiver_ref, source_ref)):
         for part in range(2):
@@ -88,7 +94,51 @@
             rows_out[0, at : at + 2, :] = ref[part, 0, 0:2, :]
             rows_out[1, at : at + 2, :] = ref[part, 0, rows - 2 : rows, :]
 
-    pl.semaphore_wait(barrier, total - 1)
+    class_out[0] = class_ref[0:1, :]
+    class_out[1] = class_ref[rows - 1 : rows, :]
+
+    lane = lax.broadcasted_iota(jnp.int32, (1, wide), 1)
+    column = jnp.where(lane < wide - wide // 4, lane, lane - wide)
+
+    def spread_of(row_step, col_step):
+        row_at = jnp.clip(strip + row_step, 0, strips - 1)
+        col_at = jnp.clip(freq + col_step, 0, groups - 1)
+        return spread_ref[col_at, row_at]
+
+    for a in range(side):
+        for b in range(side):
+            pair = psf_ref[a, b]
+            by_index[0, b, a : a + 1, 0:count] = pair[0:1] + pair[1:2]
+            by_index[1, b, a : a + 1, 0:count] = pair[0:1] - pair[1:2]
+    pick = lax.broadcasted_iota(jnp.int32, (16, share), 1)
+
+    def taps_of(st, b, chosen):
+        kept = jnp.where(pick == chosen, by_index[st, b], 0.0)
+        return jnp.sum(kept, axis=1, keepdims=True)
+
+    def fill(j, carry):
+        left = spread_of(j - near, -1)
+        middle = spread_of(j - near, 0)
+        right = spread_of(j - near, 1)
+        for st in range(2):
+            for b in range(side):
+                source_col = column - (b - reach)
+                shape = (16, wide)
+                k_left = jnp.broadcast_to(taps_of(st, b, left), shape)
+                k_middle = jnp.broadcast_to(taps_of(st, b, middle), shape)
+                k_right = jnp.broadcast_to(taps_of(st, b, right), shape)
+                table[j * 2 + st, b] = jnp.where(
+                    source_col < 0, k_left, jnp.where(source_col >= share, k_right, k_middle)
+                )
+        return carry
+
+    lax.fori_loop(0, span, fill, 0)
+    own = spread_of(0, 0)
+    for st in range(2):
+        for b in range(side):
+            own_table[st, b] = jnp.broadcast_to(taps_of(st, b, own), (16, share))
+
+    pl.semaphore_wait(barrier, groups + strips - 2)
 
     up = lax.rem(strip + strips - 1, strips)
     down = lax.rem(strip + 1, strips)
@@ -106,7 +156,7 @@
         )
         copies.append(
             pltpu.make_async_remote_copy(
-                src_ref=class_ref,
+                src_ref=class_out.at[side_at],
                 dst_ref=class_in.at[side_at],
                 send_sem=class_sem.at[side_at],
                 recv_sem=class_sem.at[2 + side_at],
@@ -116,38 +166,6 @@
         )
     for copy in copies:
         copy.start()
-
-    lane = lax.broadcasted_iota(jnp.int32, (1, wide), 1)
-    column = jnp.where(lane < wide - wide // 4, lane, lane - wide)
-
-    def spread_of(row_step, col_step):
-        row_at = jnp.clip(strip + row_step, 0, strips - 1)
-        col_at = jnp.clip(freq + col_step, 0, groups - 1)
-        chosen = spread_ref[row_at, col_at]
-        both = psf_ref[chosen]
-        return both[0] + both[1], both[0] - both[1]
-
-    def fill(j, carry):
-        left = spread_of(j - near, -1)
-        middle = spread_of(j - near, 0)
-        right = spread_of(j - near, 1)
-        for st in range(2):
-            for b in range(side):
-                source_col = column - (b - reach)
-                shape = (side, wide)
-                k_left = jnp.broadcast_to(left[st][:, b : b + 1], shape)
-                k_middle = jnp.broadcast_to(middle[st][:, b : b + 1], shape)
-                k_right = jnp.broadcast_to(right[st][:, b : b + 1], shape)
-                table[j * 2 + st, b, 0:side, :] = jnp.where(
-                    source_col < 0, k_left, jnp.where(source_col >= share, k_right, k_middle)
-                )
-        return carry
-
-    lax.fori_loop(0, span, fill, 0)
-    own = spread_of(0, 0)
-    for st in range(2):
-        for b in range(side):
-            own_table[st, b, 0:side, :] = jnp.broadcast_to(own[st][:, b : b + 1], (side, share))
 
     for field, ref in enumerate((receiver_ref, source_ref)):
         for part in range(2):
@@ -162,8 +180,8 @@
         below = rows_in[0, 2 * comp : 2 * comp + 2, :]
         fields[comp, rows - 2 : rows, :] = jnp.where(first, 0.0, above)
         fields[comp, 2 * rows : 2 * rows + 2, :] = jnp.where(last, 0.0, below)
-    classes[rows - 1 : rows, :] = class_in[1, rows - 1 : rows, :]
-    classes[2 * rows : 2 * rows + 1, :] = class_in[0, 0:1, :]
+    classes[rows - 1 : rows, :] = class_in[1]
+    classes[2 * rows : 2 * rows + 1, :] = class_in[0]
 
     levels = classes[rows - 1 : 3 * rows - 1, :]
     for part in range(2):
@@ -359,8 +377,8 @@
         return descent, image_of
 
     cells = float(STEPS * rows * strips * cols)
+    row = send_sums([migrated[0] * migrated[0] + migrated[1] * migrated[1]], 0)
     send_rim(-migrated, 0)
-    row = send_sums([migrated[0] * migrated[0] + migrated[1] * migrated[1]], 0)
     wait_all(rim_in.at[0, 0:partners], rim_sem.at[1])
     residual = rim_values(0)
     (energy,) = take_sums(row, 0, 1)
@@ -371,8 +389,6 @@
         ]
         weighted = [[w * r for w, r in zip(ws, rs)] for ws, rs in zip(weights, residual)]
         descent, image_of = descend(weighted)
-        if turn < PASSES:
-            send_rim(jnp.stack(image_of), turn)
         parts = [jnp.zeros((rows, share), jnp.float32) for q in range(4)]
         for depth in range(STEPS):
             v = image_of[depth]
@@ -384,6 +400,7 @@
             parts[3] = parts[3] + v * v
         row = send_sums(parts, turn)
         if turn < PASSES:
+            send_rim(jnp.stack(image_of), turn)
             wait_all(rim_in.at[turn, 0:partners], rim_sem.at[2 * turn + 1])
             images = rim_values(turn)
         grad_square, curvature, cross_term, power_term = take_sums(row, turn, 4)
@@ -433,13 +450,15 @@
         scratch_shapes=[
             pltpu.VMEM((2, 8, cols), f32),
             pltpu.VMEM((2, 8, cols), f32),
-            pltpu.VMEM((2, rows, cols), jnp.int32),
+            pltpu.VMEM((2, 1, cols), jnp.int32),
+            pltpu.VMEM((2, 1, cols), jnp.int32),
             pltpu.VMEM((4, 3 * rows, cols), f32),
             pltpu.VMEM((3 * rows, cols), jnp.int32),
             pltpu.VMEM((4, 3, 3 * rows, cols), f32),
             pltpu.VMEM((18, 2 * rows, cols), f32),
             pltpu.VMEM((groups, STEPS, rows, share), f32),
             pltpu.VMEM((groups - 1, STEPS, rows, share), f32),
+            pltpu.VMEM((2, side, 16, share), f32),
             pltpu.VMEM((2, side, 16, share), f32),
             pltpu.VMEM((2 * (2 * near + 1), side, 16, wide), f32),
             pltpu.VMEM((PASSES, STEPS, rows, share), f32),
@@ -457,7 +476,14 @@
             dma((2 * (PASSES + 1),)),
         ],
         compiler_params=pltpu.CompilerParams(collective_id=0, has_side_effects=True),
-    )(spread_index, filters, receiver_field, source_field, velocity_class, point_spread)
+    )(
+        spread_index.T,
+        filters,
+        receiver_field,
+        source_field,
+        velocity_class,
+        jnp.transpose(point_spread, (2, 3, 1, 0)),
+    )
     return migrated, reflectivity, misfit[0, 0]
 
 

time: 45.2 us -> 40.6 us (0.90)
  local copies, waits for them, and re-layouts: 5.2 us -> 1.9 us
  Pallas kernels: 37.3 us -> 36.1 us
    unnamed x6 -> x4, local copies, waits for them, and re-layouts: 5.2 us -> 1.9 us
    pallas_call x1, Pallas kernels: 37.3 us -> 36.1 us  [local(): pl.pallas_call(functools.partial(kernel, groups, strips, near), out_shape...]
where the time goes in v1:
time: 40.6 us; the launch traced here: 40.4 us
  Pallas kernels  36.1 us (89%)
  between operations  2.39 us (6%)
  local copies, waits for them, and re-layouts  1.9 us (5%)
    pallas_call x1, Pallas kernels, local(): pl.pallas_call(functools.partial(kernel, groups, strips, near), out_shape...  36.1 us
    unnamed x4, local copies, waits for them, and re-layouts  1.9 us

profile of v1, /device:TPU:0, one launch (start us, length us, event | category | flops | bytes accessed | tf_op | source)
XLA Modules:
  0.0 40.4 jit_solution(7497127841834838060)
XLA Ops:
  0.6 36.1 %shard_map.85 = (f32[8,2,128]{2,1,0:T(2,128)}, f32[8,2,128]{2,1,0:T(2,128)}, f32[1,1]{1,0:T(1,128)}) custom-call(s32[4,8]{1,0:T(4,128)} %bitcast.4, f32[1,8,2,9]{3,2,1,0:T(2,128)} %filters_ref.1, f32[2,1,8,512]{3,2,1,0:T(8,128)} %receiver_ref.1, f32[2,1,8,512]{3,2,1,0:T(8,128)} %source_ref.1, s32[8,512]{1,0:T(8,128)} %class_ref.1, f32[15,15,2,16]{3,2,1,0:T(2,128)} %bitcast.3), custom_call_target="tpu_custom_call" | custom-call | tf_op jit(solution)/shard_map/pallas_call | solution.py:441
  36.7 0.0 copy-start
  36.8 1.3 %copy.12 = f32[8,2,128]{2,1,0:T(2,128)} copy(f32[8,2,128]{2,1,0:T(2,128)} %get-tuple-element.12) | data formatting | bytes 16384
  38.1 0.0 copy-done
  38.1 0.6 %copy.13 = f32[8,2,128]{2,1,0:T(2,128)} copy(f32[8,2,128]{2,1,0:T(2,128)S(1)} %copy-done) | data formatting | bytes 16384
Async XLA Ops:
  36.7 1.3 %copy-start = (f32[8,2,128]{2,1,0:T(2,128)S(1)}, f32[8,2,128]{2,1,0:T(2,128)}, u32[]{:S(2)}) copy-start(f32[8,2,128]{2,1,0:T(2,128)} %get-tuple-element.13) | copy-start | bytes 24580

commit v2 on v1

--- a/solution.py
+++ b/solution.py
@@ -42,9 +42,10 @@
     table,
     rim_out,
     rim_in,
+    edge_out,
+    edge_in,
     rolled,
     spill,
-    strip_spill,
     moved,
     sums_out,
     sums_in,
@@ -52,6 +53,7 @@
     recv_sem,
     class_sem,
     rim_sem,
+    edge_sem,
     sum_sem,
 ):
     freq = lax.axis_index("freq")
@@ -67,9 +69,9 @@
     reaches = [(dj, dk) for dj in range(-near, near + 1) for dk in (-1, 0, 1)]
     reaches.remove((0, 0))
     reaches.append((0, 0))
-    place = {pair: at for at, pair in enumerate(reaches)}
-    partners = len(reaches) - 1
     span = 2 * near + 1
+    rim_place = {dj: at for at, dj in enumerate([d for d in range(-near, near + 1) if d] + [0])}
+    edge_place = {pair: at for at, pair in enumerate([p for p in reaches if p[1]])}
 
     barrier = pltpu.get_barrier_semaphore()
 
@@ -253,15 +255,26 @@
     for depth in range(STEPS):
         migrated_ref[:, depth, :] = migrated[depth]
 
+    quarter = share // 4
+    half = share // 2
+    slim = lax.broadcasted_iota(jnp.int32, (1, share), 1)
+
     def send_rim(value, turn):
         rim_out[turn] = value
-        rim_in[turn, partners] = value
+        rim_in[turn, span - 1] = value
+        far_round = pltpu.roll(value[1], half, 1)
+        edge_out[turn] = jnp.where((slim >= quarter) & (slim < share - quarter), far_round, value[0])
         for dj, dk in reaches[:-1]:
+            plain = dk == 0
+            source = rim_out if plain else edge_out
+            target = rim_in if plain else edge_in
+            sem = rim_sem if plain else edge_sem
+            slot = rim_place[-dj] if plain else edge_place[(-dj, -dk)]
             pltpu.make_async_remote_copy(
-                src_ref=rim_out.at[turn],
-                dst_ref=rim_in.at[turn, place[(-dj, -dk)]],
-                send_sem=rim_sem.at[2 * turn],
-                recv_sem=rim_sem.at[2 * turn + 1],
+                src_ref=source.at[turn],
+                dst_ref=target.at[turn, slot],
+                send_sem=sem.at[2 * turn],
+                recv_sem=sem.at[2 * turn + 1],
                 device_id=(
                     lax.rem(freq + dk + groups, groups),
                     lax.rem(strip + dj + near * strips, strips),
@@ -269,8 +282,6 @@
                 device_id_type=MESH,
             ).start()
 
-    quarter = share // 4
-    slim = lax.broadcasted_iota(jnp.int32, (1, share), 1)
 
     def send_sums(parts, turn):
         row = jnp.zeros((1, share), jnp.float32)
@@ -313,13 +324,13 @@
         for dj in range(-near, near + 1):
             ok = (strip + dj >= 0) & (strip + dj < strips)
             pair = []
+            right = jnp.where(ok & (freq < groups - 1), edge_in[turn, edge_place[(dj, 1)]], 0.0)
+            left = jnp.where(ok & (freq > 0), edge_in[turn, edge_place[(dj, -1)]], 0.0)
+            both = jnp.where(lax.rem(slim, half) < quarter, right, left)
             for depth in range(STEPS):
-                middle = jnp.where(ok, rim_in[turn, place[(dj, 0)], depth], 0.0)
-                right = jnp.where(ok & (freq < groups - 1), rim_in[turn, place[(dj, 1)], depth], 0.0)
-                left = jnp.where(ok & (freq > 0), rim_in[turn, place[(dj, -1)], depth], 0.0)
-                outer = jnp.where(
-                    slim < 2 * reach, right, jnp.where(slim >= share - 2 * reach, left, 0.0)
-                )
+                middle = jnp.where(ok, rim_in[turn, rim_place[dj], depth], 0.0)
+                outer = both if depth == 0 else pltpu.roll(both, half, 1)
+                outer = jnp.where((slim < 2 * reach) | (slim >= share - 2 * reach), outer, 0.0)
                 pair.append(jnp.concatenate([middle, outer], axis=1))
             found.append(pair)
         return found
@@ -334,24 +345,23 @@
                     rolled[2 * j + st, b] = pltpu.roll(both, (b - reach) % wide, 1)
         spill[...] = jnp.zeros_like(spill)
 
-        def one(index, carry):
-            j = index // 2
-            st = lax.rem(index, 2)
-            strip_spill[...] = jnp.zeros_like(strip_spill)
-            for low in (0, 5, 10):
-                high = min(low + 5, side)
-                totals = [jnp.zeros((rows, wide), jnp.float32) for a in range(low, high)]
-                for b in range(side):
-                    data = rolled[index, b]
-                    for a in range(low, high):
-                        totals[a - low] = totals[a - low] + table[index, b, a : a + 1, :] * data
-                for a in range(low, high):
-                    strip_spill[a : a + rows, :] += totals[a - low]
-            at = pl.ds(pl.multiple_of(rows * j, rows), tall)
-            spill[st, at, :] += strip_spill[...]
+        base = near * rows
+
+        def one(st, carry):
+            for j in range(span):
+                taps = [a for a in range(side) if base - rows < rows * j + a < base + rows + 2 * reach]
+                for low in range(0, len(taps), 5):
+                    some = taps[low : low + 5]
+                    totals = [jnp.zeros((rows, wide), jnp.float32) for a in some]
+                    for b in range(side):
+                        data = rolled[2 * j + st, b]
+                        for at, a in enumerate(some):
+                            totals[at] = totals[at] + table[2 * j + st, b, a : a + 1, :] * data
+                    for at, a in enumerate(some):
+                        spill[st, rows * j + a : rows * j + a + rows, :] += totals[at]
             return carry
 
-        lax.fori_loop(0, 2 * span, one, 0)
+        lax.fori_loop(0, 2, one, 0)
         depth_line = lax.broadcasted_iota(jnp.int32, (tall, wide), 0) - reach + strip * rows
         at_col = column + freq * share
         ok = (
@@ -360,7 +370,6 @@
             & (at_col >= 0)
             & (at_col < groups * share)
         )
-        base = near * rows
         values = [jnp.where(ok, spill[st, base : base + tall, :], 0.0) for st in range(2)]
         for st in range(2):
             spill[st, base : base + tall, :] = values[st]
@@ -379,7 +388,8 @@
     cells = float(STEPS * rows * strips * cols)
     row = send_sums([migrated[0] * migrated[0] + migrated[1] * migrated[1]], 0)
     send_rim(-migrated, 0)
-    wait_all(rim_in.at[0, 0:partners], rim_sem.at[1])
+    wait_all(rim_in.at[0, 0 : span - 1], rim_sem.at[1])
+    wait_all(edge_in.at[0], edge_sem.at[1])
     residual = rim_values(0)
     (energy,) = take_sums(row, 0, 1)
     reflect = [jnp.zeros((rows, share), jnp.float32) for depth in range(STEPS)]
@@ -401,7 +411,8 @@
         row = send_sums(parts, turn)
         if turn < PASSES:
             send_rim(jnp.stack(image_of), turn)
-            wait_all(rim_in.at[turn, 0:partners], rim_sem.at[2 * turn + 1])
+            wait_all(rim_in.at[turn, 0 : span - 1], rim_sem.at[2 * turn + 1])
+            wait_all(edge_in.at[turn], edge_sem.at[2 * turn + 1])
             images = rim_values(turn)
         grad_square, curvature, cross_term, power_term = take_sums(row, turn, 4)
         step_length = grad_square / curvature
@@ -417,7 +428,8 @@
 
     wait_all(terms_in, send_sem.at[2])
     for turn in range(PASSES):
-        wait_all(rim_in.at[turn, 0:partners], rim_sem.at[2 * turn])
+        wait_all(rim_in.at[turn, 0 : span - 1], rim_sem.at[2 * turn])
+        wait_all(edge_in.at[turn], edge_sem.at[2 * turn])
     for turn in range(PASSES + 1):
         wait_all(sums_in.at[turn], sum_sem.at[2 * turn])
 
@@ -430,7 +442,6 @@
     side = point_spread.shape[2]
     reach = side // 2
     near = -(-2 * reach // rows)
-    partners = 3 * (2 * near + 1) - 1
     total = groups * strips
     wide = 2 * share
     vmem = pl.BlockSpec(memory_space=pltpu.VMEM)
@@ -462,16 +473,18 @@
             pltpu.VMEM((2, side, 16, share), f32),
             pltpu.VMEM((2 * (2 * near + 1), side, 16, wide), f32),
             pltpu.VMEM((PASSES, STEPS, rows, share), f32),
-            pltpu.VMEM((PASSES, partners + 1, STEPS, rows, share), f32),
+            pltpu.VMEM((PASSES, 2 * near + 1, STEPS, rows, share), f32),
+            pltpu.VMEM((PASSES, rows, share), f32),
+            pltpu.VMEM((PASSES, 2 * (2 * near + 1), rows, share), f32),
             pltpu.VMEM((2 * (2 * near + 1), side, rows, wide), f32),
             pltpu.VMEM((2, deep, wide), f32),
-            pltpu.VMEM((3 * rows, wide), f32),
             pltpu.VMEM((2, side, 3 * rows, share), f32),
             pltpu.VMEM((PASSES + 1, 1, share), f32),
             pltpu.VMEM((PASSES + 1, total - 1, 1, share), f32),
             dma((3,)),
             dma((3,)),
             dma((4,)),
+            dma((2 * PASSES,)),
             dma((2 * PASSES,)),
             dma((2 * (PASSES + 1),)),
         ],

time: 40.6 us -> 38.2 us (0.941)
  Pallas kernels: 36.1 us -> 33.7 us
    pallas_call x1, Pallas kernels: 36.1 us -> 33.7 us  [local(): pl.pallas_call(functools.partial(kernel, groups, strips, near), out_shape...]
where the time goes in v2:
time: 38.2 us; the launch traced here: 38 us
  Pallas kernels  33.7 us (88%)
  between operations  2.39 us (6%)
  local copies, waits for them, and re-layouts  1.9 us (5%)
    pallas_call x1, Pallas kernels, local(): pl.pallas_call(functools.partial(kernel, groups, strips, near), out_shape...  33.7 us
    unnamed x4, local copies, waits for them, and re-layouts  1.9 us

profile of v2, /device:TPU:0, one launch (start us, length us, event | category | flops | bytes accessed | tf_op | source)
XLA Modules:
  0.0 38.0 jit_solution(353768190566174702)
XLA Ops:
  0.6 33.7 %shard_map.85 = (f32[8,2,128]{2,1,0:T(2,128)}, f32[8,2,128]{2,1,0:T(2,128)}, f32[1,1]{1,0:T(1,128)}) custom-call(s32[4,8]{1,0:T(4,128)} %bitcast.4, f32[1,8,2,9]{3,2,1,0:T(2,128)} %filters_ref.1, f32[2,1,8,512]{3,2,1,0:T(8,128)} %receiver_ref.1, f32[2,1,8,512]{3,2,1,0:T(8,128)} %source_ref.1, s32[8,512]{1,0:T(8,128)} %class_ref.1, f32[15,15,2,16]{3,2,1,0:T(2,128)} %bitcast.3), custom_call_target="tpu_custom_call" | custom-call | tf_op jit(solution)/shard_map/pallas_call | solution.py:452
  34.3 0.0 copy-start
  34.3 1.3 %copy.12 = f32[8,2,128]{2,1,0:T(2,128)} copy(f32[8,2,128]{2,1,0:T(2,128)} %get-tuple-element.12) | data formatting | bytes 16384
  35.6 0.0 copy-done
  35.6 0.6 %copy.13 = f32[8,2,128]{2,1,0:T(2,128)} copy(f32[8,2,128]{2,1,0:T(2,128)S(1)} %copy-done) | data formatting | bytes 16384
Async XLA Ops:
  34.3 1.3 %copy-start = (f32[8,2,128]{2,1,0:T(2,128)S(1)}, f32[8,2,128]{2,1,0:T(2,128)}, u32[]{:S(2)}) copy-start(f32[8,2,128]{2,1,0:T(2,128)} %get-tuple-element.13) | copy-start | bytes 24580
